TPU v7x, 32 devices: a whole 2x2x4 slice. The times are simulated.
32 devices in a mesh: gx: 16 (over z, x, core), gy: 2 (over y).
Axes of the slice: x: 2, y: 2, z: 4, core: 2. Of those that a mesh axis runs over, the one named last changes fastest.
Arguments:
- prefix_tokens: bfloat16 [12288, 8192], P('gx'), may hold values from -6 to 6
- key_value_weight: bfloat16 [8192, 2048], P('gx', 'gy'), may hold values from -0.0625 to 0.0625
- prefix_lengths: int32 [96], P('gx'), may hold values from 1 to 128, as said below
- start_offsets: int32 [96], P('gx'), may hold values from 0 to 1920
- queries: bfloat16 [4, 8192], P('gy'), may hold values from -5 to 5
- key_value_cache: bfloat16 [2, 4, 2048, 1024], P(None, 'gy', 'gx'), may hold values from -5 to 5
- cache_lengths: int32 [4], P('gy'), may hold values from 256 to 2048, as said below
- out_weight: bfloat16 [8192, 8192], P('gy', 'gx'), may hold values from -0.5 to 0.5
Outputs:
- prefix_kv: bfloat16 [12288, 2048], P('gx', 'gy')
- decode_out: bfloat16 [4, 8192], P('gy', 'gx')
Inputs may be any that keep to these rules, and one draw needn't show every extreme that they name: `prefix_lengths`: live tokens stand at the front of a prefix's slots; in every draw some prefix uses all 128 slots. `cache_lengths`: live positions stand at the front of a trajectory's cache; in every draw some trajectory uses all 2048 positions.
All inputs are finite; a program needn't handle non-finite values.
Results may differ from a plain program's by a relative error of at most 0.0051.
Values may be sent and summed in bfloat16 or wider, within the bound.
A program may use at most 64 MiB of HBM per device.

v0:
```python
import jax
import jax.numpy as jnp
from jax import lax
from jax.sharding import PartitionSpec as P

QUERY_HEADS = 64
KEY_VALUE_HEADS = 8
HEAD_SIZE = 128
SLOT = 128


rope_base = 500000.0
masked_score = -1e30


def merged(part, axis, combine):
    gathered = jax.tree.map(lambda a: lax.all_gather(a, axis), part)

    def take(source):
        return jax.tree.map(lambda a: lax.dynamic_index_in_dim(a, source, 0, False), gathered)

    return lax.fori_loop(
        1, lax.axis_size(axis), lambda source, state: combine(state, take(source)), take(0)
    )


def rotate_and_mask(projected, first_column, prefix_lengths, start_offsets):
    tok_rows, columns = projected.shape
    slot_index = jnp.arange(SLOT, dtype=jnp.int32)
    positions = (start_offsets[:, None] + slot_index[None, :]).reshape(tok_rows)
    live_rows = (slot_index[None, :] < prefix_lengths[:, None]).reshape(tok_rows)
    half_width = HEAD_SIZE // 2
    freq_index = jnp.arange(half_width, dtype=jnp.float32)
    inverse = rope_base ** (-2.0 * freq_index / HEAD_SIZE)
    angles = positions.astype(jnp.float32)[:, None] * inverse[None, :]
    cosine = jnp.cos(angles)[:, None, :]
    sine = jnp.sin(angles)[:, None, :]
    head_list = projected.reshape(tok_rows, columns // HEAD_SIZE, HEAD_SIZE)
    first_half = head_list[:, :, :half_width]
    second_half = head_list[:, :, half_width:]
    rotary_applied = jnp.concatenate(
        [first_half * cosine - second_half * sine, second_half * cosine + first_half * sine], axis=2
    )
    head_position = first_column // HEAD_SIZE + jnp.arange(columns // HEAD_SIZE, dtype=jnp.int32)
    key_tagged = jnp.where(
        (head_position < KEY_VALUE_HEADS)[None, :, None], rotary_applied, head_list
    )
    kept = jnp.where(live_rows[:, None, None], key_tagged, 0.0)
    return kept.reshape(tok_rows, columns).astype(jnp.bfloat16)


def merge_parts(earlier, later):
    highest = jnp.maximum(earlier[0], later[0])
    early_factor = jnp.exp(earlier[0] - highest)
    late_factor = jnp.exp(later[0] - highest)
    summed = earlier[1] * early_factor + later[1] * late_factor
    weighted = earlier[2] * early_factor[..., None] + later[2] * late_factor[..., None]
    return (highest, summed, weighted)


def shards(
    prefix_tokens,
    key_value_weight,
    prefix_lengths,
    start_offsets,
    queries,
    key_value_cache,
    cache_lengths,
    out_weight,
):
    columns = key_value_weight.shape[1]
    projected = jnp.dot(
        prefix_tokens,
        lax.all_gather(key_value_weight, "gx", axis=0, tiled=True),
        preferred_element_type=jnp.float32,
    )
    prefix_kv = rotate_and_mask(
        projected, lax.axis_index("gy") * columns, prefix_lengths, start_offsets
    )
    trajectory_per_shard = queries.shape[0]
    cache_per_shard = key_value_cache.shape[2]
    query_group = QUERY_HEADS // KEY_VALUE_HEADS
    query_head_rows = queries.reshape(trajectory_per_shard, KEY_VALUE_HEADS, query_group, HEAD_SIZE)
    key_rows = key_value_cache[0].reshape(
        trajectory_per_shard, cache_per_shard, KEY_VALUE_HEADS, HEAD_SIZE
    )
    value_rows = key_value_cache[1].reshape(
        trajectory_per_shard, cache_per_shard, KEY_VALUE_HEADS, HEAD_SIZE
    )
    scores = jnp.einsum(
        "bhgd,bphd->bhgp", query_head_rows, key_rows, preferred_element_type=jnp.float32
    ) * HEAD_SIZE ** (-0.5)
    position = lax.axis_index("gx") * cache_per_shard + jnp.arange(cache_per_shard, dtype=jnp.int32)
    valid = (position[None, :] < cache_lengths[:, None])[:, None, None, :]
    peak = jnp.max(jnp.where(valid, scores, masked_score), axis=3)
    weights = jnp.where(valid, jnp.exp(scores - peak[..., None]), 0.0)
    block_total = jnp.sum(weights, axis=3)
    numerator = jnp.einsum(
        "bhgp,bphd->bhgd",
        weights.astype(jnp.bfloat16),
        value_rows,
        preferred_element_type=jnp.float32,
    )
    peak, block_total, numerator = merged((peak, block_total, numerator), "gx", merge_parts)
    attention = (
        (numerator / block_total[..., None])
        .reshape(trajectory_per_shard, QUERY_HEADS * HEAD_SIZE)
        .astype(jnp.bfloat16)
    )
    spread = lax.all_to_all(attention, "gy", split_axis=1, concat_axis=0, tiled=True)
    partial_value = jnp.dot(spread, out_weight, preferred_element_type=jnp.float32)
    whole = lax.psum(partial_value, "gy")
    mixed = lax.dynamic_slice_in_dim(
        whole, lax.axis_index("gy") * trajectory_per_shard, trajectory_per_shard, 0
    )
    return (prefix_kv, mixed.astype(jnp.bfloat16))


def solution(mesh):
    return jax.shard_map(
        shards,
        mesh=mesh,
        in_specs=(
            P("gx", None),
            P("gx", "gy"),
            P("gx"),
            P("gx"),
            P("gy", None),
            P(None, "gy", "gx", None),
            P("gy"),
            P("gy", "gx"),
        ),
        out_specs=(P("gx", "gy"), P("gy", "gx")),
        check_vma=False,
    )
```

profile of v0, /device:TPU:0, one launch (start us, length us, event | category | flops | bytes accessed | tf_op | source)
XLA Modules:
  0.0 209.2 jit_solution(12496277527320128071)
XLA Ops:
  7.2 0.0 all-gather.8.cloned.1.call-start
  7.3 1.3 fusion.17
  8.6 0.3 copy.22
  8.8 0.3 copy.23
  9.1 0.1 broadcast_compare_fusion
  9.2 0.3 select_reduce_fusion
  9.5 1.1 fusion.7
  10.6 0.0 all-gather.8.cloned.1.call-update
  10.6 0.0 all-gather.6.cloned.1.call-start
  10.7 0.7 all-gather.6.cloned.1.call-update
  11.4 23.6 %all-gather = f32[32,8,8]{2,1,0:T(8,128)S(1)} all-gather(f32[2,8,8]{2,1,0:T(8,128)S(1)} %get-tuple-element.205), channel_id=2, replica_groups=mesh['gx'=16,'gy'=2] {'gx'}, dimensions={0}, use_global_device_ids=true | all-gather | bytes 8704 | tf_op jit(solution)/shard_map/all_gather | solution.py:17
  35.0 0.2 fusion.6
  35.1 17.8 %all-gather.1 = f32[32,8,8]{2,1,0:T(8,128)S(1)} all-gather(f32[2,8,8]{2,1,0:T(8,128)S(1)} %fusion.6), channel_id=3, replica_groups=mesh['gx'=16,'gy'=2] {'gx'}, dimensions={0}, use_global_device_ids=true | all-gather | bytes 8704 | tf_op jit(solution)/shard_map/all_gather | solution.py:17
  53.0 0.1 fusion.14
  53.1 0.1 convert_bitcast_fusion
  53.2 1.4 multiply_cosine_fusion
  54.6 0.0 all-gather.8.cloned.1.call-done
  54.6 0.8 slice.26
  55.5 15.1 %while.19 = (s32[]{:T(128)}, f32[2,8,8]{2,1,0:T(8,128)S(1)}, f32[2,8,8]{2,1,0:T(8,128)S(1)}, f32[2,8,8,128]{3,2,1,0:T(8,128)S(1)}, f32[16,2,8,8]{3,2,1,0:T(8,128...) while((s32[]{:T(128)}, f32[2,8,8]{2,1,0:T(8,128)S(1)}, ...), condition=%wide.region_3.4_spmd, body=%wide.region_2.3_spmd.sunk | while | flops 49925 | bytes 201879 | solution.py:22
  55.5 1.0 fusion.29
  56.5 1.0 fusion.29
  57.5 1.0 fusion.29
  58.5 1.0 fusion.29
  59.5 1.0 fusion.29
  60.5 1.0 fusion.29
  61.6 1.0 fusion.29
  62.6 1.0 fusion.29
  63.6 1.0 fusion.29
  64.6 1.0 fusion.29
  65.6 1.0 fusion.29
  66.6 1.0 fusion.29
  67.6 1.0 fusion.29
  68.6 1.0 fusion.29
  69.6 1.0 fusion.29
  70.6 0.1 divide_convert_fusion
  70.7 0.6 copy.19
  71.4 3.3 %all-to-all-start = ((bf16[2,2,4096]{2,0,1:T(2,128)(2,1)}), bf16[2,2,4096]{2,0,1:T(2,128)(2,1)S(1)}, u32[]{:S(2)}, u32[]{:S(2)}) async-start(bf16[2,2,4096]{2,0,1:T(2,128)(2,1)} %copy.19), calls=%async_computation | async-start | bytes 65536 | tf_op jit(solution)/shard_map/all_to_all | solution.py:110
  74.6 0.1 broadcast_bitcast_fusion
  74.7 3.9 %all-to-all-done = bf16[2,2,4096]{2,0,1:T(2,128)(2,1)S(1)} async-done(((bf16[2,2,4096]{2,0,1:T(2,128)(2,1)}), bf16[2,2,4096]{2,0,1:T(2,128)(2,1)S(1)}, u32[]{:S(2)}, u32[]{:S(2)}) %all-to-all-start) | async-done | bytes 32800 | tf_op jit(solution)/shard_map/all_to_all | solution.py:110
  78.6 2.8 %fusion.19 = f32[4,512]{1,0:T(4,128)S(1)} fusion(bf16[4,4096]{1,0:T(4,128)(2,1)S(1)} %all_to_all.14, bf16[4096,512]{1,0:T(8,128)(2,1)} %param.17), kind=kOutput, calls=%fused_computation.40 | convolution fusion | flops 16777216 | bytes 4235264 | tf_op jit(solution)/shard_map/dot_general | solution.py:111
  81.4 5.0 %psum.7 = bf16[4,512]{1,0:T(4,128)(2,1)S(1)} all-reduce(f32[4,512]{1,0:T(4,128)S(1)} %fusion.19), channel_id=1, replica_groups=mesh['gx'=16,'gy'=2] {'gy'}, use_global_device_ids=true, to_apply=%region_4.5 | all-reduce | flops 2048 | bytes 12288 | tf_op jit(solution)/shard_map/psum | solution.py:112
  86.4 0.6 dynamic-slice_convert_fusion
  87.0 92.1 %all-gather.6.cloned.1.call-done = bf16[8192,1024]{1,0:T(8,128)(2,1)} async-done(((bf16[512,1024]{1,0:T(8,128)(2,1)}), bf16[8192,1024]{1,0:T(8,128)(2,1)}) %all-gather.6.cloned.1.call-update) | async-done | bytes 16777232 | tf_op jit(solution)/shard_map/all_gather | solution.py:74
  179.1 18.6 %fusion.18 = f32[768,1024]{1,0:T(8,128)S(1)} fusion(bf16[768,8192]{1,0:T(8,128)(2,1)} %param.10, bf16[8192,1024]{1,0:T(8,128)(2,1)} %all-gather.6.cloned.1.call-done), kind=kOutput, calls=%fused_computation.39 | convolution fusion | flops 12884901888 | bytes 32505856 | tf_op jit(solution)/shard_map/dot_general | solution.py:72
  197.7 0.7 copy.24
  198.5 1.5 multiply_subtract_fusion
  200.0 0.9 pad_maximum_fusion
  200.8 1.5 fusion.4
  (30 shorter events, 0.4 us)
Async XLA Ops:
  7.2 1.9 copy-start.2
  7.2 2.0 copy-start
  7.2 47.4 %all-gather.8.cloned.1.call-start = ((), (), s32[]{:S(2)}) async-start(), calls=%async_computation.2 | async-start | bytes 1114112 | tf_op jit(solution)/shard_map/all_gather | solution.py:17
  7.2 45.8 %copy-start.3 = (s32[6]{0:T(128)S(1)}, s32[6]{0:T(128)}, u32[]{:S(2)}) copy-start(s32[6]{0:T(128)} %param.12) | copy-start | bytes 76
  7.3 45.8 %copy-start.1 = (s32[6]{0:T(128)S(1)}, s32[6]{0:T(128)}, u32[]{:S(2)}) copy-start(s32[6]{0:T(128)} %param.13) | copy-start | bytes 76
  10.6 168.5 %all-gather.6.cloned.1.call-start = ((), (), s32[]{:S(2)}) async-start(), calls=%async_computation.1 | async-start | bytes 17825792 | tf_op jit(solution)/shard_map/all_gather | solution.py:74
  71.4 7.2 %all-to-all-start = ((bf16[2,2,4096]{2,0,1:T(2,128)(2,1)}), bf16[2,2,4096]{2,0,1:T(2,128)(2,1)S(1)}, u32[]{:S(2)}, u32[]{:S(2)}) async-start(bf16[2,2,4096]{2,0,1:T(2,128)(2,1)} %copy.19), calls=%async_computation | async-start | bytes 65536 | tf_op jit(solution)/shard_map/all_to_all | solution.py:110
Sparse Core Ops, SparseCore 0:
  10.7 40.7 all-gather.7
  53.7 125.4 all-gather.5
where the time goes:
time: 210 us; the launch traced here: 209 us
  waiting for transfers between devices  96.7 us (46%)
  blocking collectives  46.4 us (22%)
  matrix products  22.8 us (11%)
  other arithmetic  20.5 us (10%)
  between operations  14.2 us (7%)
  local copies, waits for them, and re-layouts  4.77 us (2%)
  starting transfers between devices  3.34 us (2%)
    all_gather x1, waiting for transfers between devices, shards(): lax.all_gather(key_value_weight, 'gx', axis=0, tiled=True)  92.1 us
    all_gather x2, blocking collectives, merged(): gathered = jax.tree.map(lambda a: lax.all_gather(a, axis), part)  41.4 us
    dot_general x1, matrix products, shards(): jnp.dot(prefix_tokens, lax.all_gather(key_value_weight, 'gx', axis=0, til...  18.6 us
    add x15, other arithmetic, merge_parts(): earlier[2] * early_factor[..., None] + later[2] * late_factor[..., None]  14.4 us
    psum x1, blocking collectives, shards(): whole = lax.psum(partial_value, 'gy')  4.98 us
  transfers between devices with their start and end apart: 3, of which 2 were waited for; matrix products, arithmetic and copies ran while one was open for 10% of the time, Pallas kernels for 0%

commit v1 on v0

--- a/solution.py
+++ b/solution.py
@@ -1,12 +1,17 @@
+import functools
+
 import jax
 import jax.numpy as jnp
 from jax import lax
+from jax.experimental import pallas as pl
+from jax.experimental.pallas import tpu as pltpu
 from jax.sharding import PartitionSpec as P
 
 QUERY_HEADS = 64
 KEY_VALUE_HEADS = 8
 HEAD_SIZE = 128
 SLOT = 128
+MESH = pl.DeviceIdType.MESH
 
 
 rope_base = 500000.0
@@ -24,29 +29,326 @@
     )
 
 
-def rotate_and_mask(projected, first_column, prefix_lengths, start_offsets):
-    tok_rows, columns = projected.shape
+def plane_of(mesh):
+    n = mesh.shape["gx"]
+    line = list(mesh.devices[:, 0])
+    where = [tuple(getattr(d, "coords", (i, 0, i))) for i, d in enumerate(line)]
+    nc = 1
+    while nc < n and where[nc] == where[0]:
+        nc += 1
+    row = 1
+    while row < n and where[row][2] == where[0][2]:
+        row += 1
+    if row % nc or n % row:
+        return n, 1, 1
+    return n // row, row // nc, nc
+
+
+def prefill_kernel(
+    plane, groups, direct, x_hbm, w_hbm, cos_ref, sin_ref, mask_ref, o_ref,
+    xbuf, wbuf, x_sem, own_sem, recv_sem, up_sem, down_sem, cross_sem, core_sem,
+):
+    nz, nx, nc = plane
+    me = lax.axis_index("gx")
+    key_groups = KEY_VALUE_HEADS - lax.axis_index("gy") * groups
+    z = lax.div(me, nx * nc)
+    x = lax.rem(lax.div(me, nc), nx)
+    c = lax.rem(me, nc)
+    depth = w_hbm.shape[0]
+    rows = x_hbm.shape[0]
+    tile = 256
+    tiles = rows // tile
+    travelled = groups - direct
+
+    def index(zz, xx, cc):
+        return (zz * nx + xx) * nc + cc
+
+    def piece(g, block):
+        return wbuf.at[g, pl.ds(pl.multiple_of(block * depth, depth), depth), :]
+
+    def remote(g, block, sem, target):
+        return pltpu.make_async_remote_copy(
+            src_ref=piece(g, block), dst_ref=piece(g, block), send_sem=sem,
+            recv_sem=recv_sem.at[g, block], device_id={"gx": target}, device_id_type=MESH,
+        )
+
+    def arrived(g, block):
+        remote(g, block, up_sem.at[0, 0], me).wait_recv()
+
+    def plane_block(block):
+        return lax.div(block, nc)
+
+    def send_up(g, block, act):
+        @pl.when(z < nz - 1)
+        def _():
+            act(remote(g, block, up_sem.at[g, plane_block(block)], index(z + 1, x, c)))
+
+    def send_down(g, block, act):
+        @pl.when(z > 0)
+        def _():
+            act(remote(g, block, down_sem.at[g, plane_block(block)], index(z - 1, x, c)))
+
+    def send_cross(g, block, act):
+        for step in range(1, nx):
+            act(remote(g, block, cross_sem.at[g, plane_block(block), step - 1], index(z, lax.rem(x + step, nx), c)))
+
+    def send_core(g, block, act):
+        for step in range(1, nc):
+            act(remote(g, block, core_sem.at[g, plane_block(block), step - 1], index(z, x, lax.rem(c + step, nc))))
+
+    start = lambda copy: copy.start()
+    finish = lambda copy: copy.wait_send()
+
+    def own_copy(g):
+        return pltpu.make_async_copy(w_hbm.at[:, pl.ds(pl.multiple_of(g * HEAD_SIZE, HEAD_SIZE), HEAD_SIZE)], piece(g, me), own_sem.at[g])
+
+    def each(low, high, body):
+        lax.fori_loop(low, high, lambda i, s: (body(i), s)[1], 0)
+
+    x_copy = pltpu.make_async_copy(x_hbm, xbuf, x_sem)
+    if direct:
+        own_copy(groups - 1).start()
+    each(0, travelled, lambda g: own_copy(g).start())
+    x_copy.start()
+
+    barrier = pltpu.get_barrier_semaphore()
+
+    def greet(target):
+        pl.semaphore_signal(barrier, inc=1, device_id={"gx": target}, device_id_type=MESH)
+
+    @pl.when(z > 0)
+    def _():
+        greet(index(z - 1, x, c))
+
+    @pl.when(z < nz - 1)
+    def _():
+        greet(index(z + 1, x, c))
+
+    for step in range(1, nx):
+        greet(index(z, lax.rem(x + step, nx), c))
+    for step in range(1, nc):
+        greet(index(z, x, lax.rem(c + step, nc)))
+
+    peers = nx + nc - 2 + jnp.where(z > 0, 1, 0) + jnp.where(z < nz - 1, 1, 0)
+    pl.semaphore_wait(barrier, peers)
+
+    def send_own(g, act):
+        send_up(g, me, act)
+        send_down(g, me, act)
+        send_cross(g, me, act)
+        send_core(g, me, act)
+
+    def ready_own(g):
+        own_copy(g).wait()
+        send_own(g, start)
+
+    last = groups - 1
+    ahead = min(2, travelled)
+    ready_own(jnp.int32(0))
+    if direct:
+        ready_own(jnp.int32(last))
+    each(1, ahead, ready_own)
+
+    def from_z(g, zs, xs, crossing, act):
+        block = index(zs, xs, c)
+
+        @pl.when(zs < z)
+        def _():
+            send_up(g, block, act)
+
+        @pl.when(zs > z)
+        def _():
+            send_down(g, block, act)
+
+        if crossing:
+            send_cross(g, block, act)
+        send_core(g, block, act)
+
+    def both_sides(d, body):
+        @pl.when(z >= d)
+        def _():
+            body(z - d)
+
+        @pl.when(z + d < nz)
+        def _():
+            body(z + d)
+
+    def take_z(g, d):
+        def side(zs):
+            arrived(g, index(zs, x, c))
+            from_z(g, zs, x, True, start)
+
+        both_sides(d, side)
+
+    def take_x(g):
+        for step in range(1, nx):
+            def one(zs, step=step):
+                block = index(zs, lax.rem(x + step, nx), c)
+                arrived(g, block)
+                send_core(g, block, start)
+
+            each(0, nz, one)
+
+    def take_core(g):
+        for step in range(1, nc):
+            def one(chip, step=step):
+                arrived(g, chip * nc + lax.rem(c + step, nc))
+
+            each(0, nz * nx, one)
+
+    def direct_first(act, waiting):
+        for step in range(1, nx):
+            block = index(z, lax.rem(x + step, nx), c)
+            if waiting:
+                arrived(last, block)
+            send_up(last, block, act)
+            send_down(last, block, act)
+            send_core(last, block, act)
+
+    def direct_z(s, act, waiting):
+        d = 1 + lax.div(s, nx)
+        xs = lax.rem(x + lax.rem(s, nx), nx)
+
+        def side(zs):
+            if waiting:
+                arrived(last, index(zs, xs, c))
+            from_z(last, zs, xs, False, act)
+
+        both_sides(d, side)
+
+    def multiply(g, r):
+        span = pl.ds(pl.multiple_of(r * tile, tile), tile)
+        value = jnp.dot(xbuf[span, :], wbuf[g], preferred_element_type=jnp.float32)
+        turned = value * cos_ref[span, :] + pltpu.roll(value, HEAD_SIZE // 2, 1) * sin_ref[span, :]
+        value = jnp.where(g < key_groups, turned, value)
+        value = jnp.where(mask_ref[span, :] > 0.0, value, 0.0)
+        o_ref[span, pl.ds(pl.multiple_of(g * HEAD_SIZE, HEAD_SIZE), HEAD_SIZE)] = value.astype(o_ref.dtype)
+
+    x_copy.wait()
+
+    def step(g):
+        @pl.when(g + ahead < travelled)
+        def _():
+            ready_own(g + ahead)
+
+        @pl.when(g >= 2)
+        def _():
+            take_core(g - 2)
+
+        if direct:
+            @pl.when(g == 0)
+            def _():
+                direct_first(start, True)
+
+        def hop(d):
+            take_z(g, d)
+
+            @pl.when(jnp.logical_and(g >= 2, d <= tiles))
+            def _():
+                multiply(g - 2, d - 1)
+
+        each(1, nz, hop)
+
+        @pl.when(g >= 2)
+        def _():
+            each(min(nz - 1, tiles), tiles, lambda r: multiply(g - 2, r))
+
+        @pl.when(g >= 1)
+        def _():
+            take_x(g - 1)
+
+        if direct:
+            @pl.when(g < (nz - 1) * nx)
+            def _():
+                direct_z(g, start, True)
+
+    each(0, travelled, step)
+
+    def whole(g):
+        take_core(g)
+        each(0, tiles, lambda r: multiply(g, r))
+
+    def finish_group(i):
+        g = i
+
+        @pl.when(i == travelled - 1)
+        def _():
+            take_x(i)
+
+        whole(g)
+
+    if direct:
+        order_low = max(travelled - 2, 0)
+        def closing(i):
+            g = lax.rem(i + 1, 3)
+            g = jnp.where(i == 0, last, order_low + i - 1)
+            @pl.when(i == 2)
+            def _():
+                take_x(g)
+            whole(g)
+        each(0, 3, closing)
+    else:
+        each(max(travelled - 2, 0), travelled, finish_group)
+
+    def sent(g):
+        send_own(g, finish)
+
+        def hop(d):
+            both_sides(d, lambda zs: from_z(g, zs, x, True, finish))
+
+        each(1, nz, hop)
+        for step in range(1, nx):
+            each(0, nz, lambda zs, step=step: send_core(g, index(zs, lax.rem(x + step, nx), c), finish))
+
+    each(0, travelled, sent)
+    if direct:
+        send_own(last, finish)
+        direct_first(finish, False)
+        each(0, (nz - 1) * nx, lambda s: direct_z(s, finish, False))
+
+
+def prefill(plane, tokens, weight, prefix_lengths, start_offsets):
+    nz, nx, nc = plane
+    n = nz * nx * nc
+    rows = tokens.shape[0]
+    depth, columns = weight.shape
+    groups = columns // HEAD_SIZE
+    direct = 1 if groups >= 6 and nx > 1 and (nz - 1) * nx < groups else 0
     slot_index = jnp.arange(SLOT, dtype=jnp.int32)
-    positions = (start_offsets[:, None] + slot_index[None, :]).reshape(tok_rows)
-    live_rows = (slot_index[None, :] < prefix_lengths[:, None]).reshape(tok_rows)
-    half_width = HEAD_SIZE // 2
-    freq_index = jnp.arange(half_width, dtype=jnp.float32)
-    inverse = rope_base ** (-2.0 * freq_index / HEAD_SIZE)
+    positions = (start_offsets[:, None] + slot_index[None, :]).reshape(rows)
+    live = (slot_index[None, :] < prefix_lengths[:, None]).reshape(rows)
+    half = HEAD_SIZE // 2
+    inverse = rope_base ** (-2.0 * jnp.arange(half, dtype=jnp.float32) / HEAD_SIZE)
     angles = positions.astype(jnp.float32)[:, None] * inverse[None, :]
-    cosine = jnp.cos(angles)[:, None, :]
-    sine = jnp.sin(angles)[:, None, :]
-    head_list = projected.reshape(tok_rows, columns // HEAD_SIZE, HEAD_SIZE)
-    first_half = head_list[:, :, :half_width]
-    second_half = head_list[:, :, half_width:]
-    rotary_applied = jnp.concatenate(
-        [first_half * cosine - second_half * sine, second_half * cosine + first_half * sine], axis=2
-    )
-    head_position = first_column // HEAD_SIZE + jnp.arange(columns // HEAD_SIZE, dtype=jnp.int32)
-    key_tagged = jnp.where(
-        (head_position < KEY_VALUE_HEADS)[None, :, None], rotary_applied, head_list
-    )
-    kept = jnp.where(live_rows[:, None, None], key_tagged, 0.0)
-    return kept.reshape(tok_rows, columns).astype(jnp.bfloat16)
+    cosine, sine = jnp.cos(angles), jnp.sin(angles)
+    cosine = jnp.concatenate([cosine, cosine], axis=1)
+    sine = jnp.concatenate([-sine, sine], axis=1)
+    mask = jnp.broadcast_to(live[:, None], (rows, HEAD_SIZE)).astype(jnp.float32)
+    chips = nz * nx
+    vmem = pl.BlockSpec(memory_space=pltpu.VMEM)
+    anywhere = pl.BlockSpec(memory_space=pl.ANY)
+    dma = pltpu.SemaphoreType.DMA
+    return pl.pallas_call(
+        functools.partial(prefill_kernel, plane, groups, direct),
+        out_shape=jax.ShapeDtypeStruct((rows, columns), jnp.bfloat16),
+        in_specs=[anywhere, anywhere, vmem, vmem, vmem],
+        out_specs=vmem,
+        scratch_shapes=[
+            pltpu.VMEM(tokens.shape, jnp.bfloat16),
+            pltpu.VMEM((groups, n * depth, HEAD_SIZE), jnp.bfloat16),
+            dma(()),
+            dma((groups,)),
+            dma((groups, n)),
+            dma((groups, chips)),
+            dma((groups, chips)),
+            dma((groups, chips, max(nx - 1, 1))),
+            dma((groups, chips, max(nc - 1, 1))),
+        ],
+        compiler_params=pltpu.CompilerParams(
+            collective_id=0, has_side_effects=True, vmem_limit_bytes=48 * 1024 * 1024
+        ),
+        name="prefill",
+    )(tokens, weight, cosine, sine, mask)
 
 
 def merge_parts(earlier, later):
@@ -59,6 +361,7 @@
 
 
 def shards(
+    plane,
     prefix_tokens,
     key_value_weight,
     prefix_lengths,
@@ -68,15 +371,7 @@
     cache_lengths,
     out_weight,
 ):
-    columns = key_value_weight.shape[1]
-    projected = jnp.dot(
-        prefix_tokens,
-        lax.all_gather(key_value_weight, "gx", axis=0, tiled=True),
-        preferred_element_type=jnp.float32,
-    )
-    prefix_kv = rotate_and_mask(
-        projected, lax.axis_index("gy") * columns, prefix_lengths, start_offsets
-    )
+    prefix_kv = prefill(plane, prefix_tokens, key_value_weight, prefix_lengths, start_offsets)
     trajectory_per_shard = queries.shape[0]
     cache_per_shard = key_value_cache.shape[2]
     query_group = QUERY_HEADS // KEY_VALUE_HEADS
@@ -118,7 +413,7 @@
 
 def solution(mesh):
     return jax.shard_map(
-        shards,
+        functools.partial(shards, plane_of(mesh)),
         mesh=mesh,
         in_specs=(
             P("gx", None),

time: 210 us -> 194 us (0.924)
  Pallas kernels: 0 us -> 102 us
  waiting for transfers between devices: 96.7 us -> 0.04 us
  matrix products: 22.8 us -> 4.21 us
  other arithmetic: 20.5 us -> 16.8 us
    pallas_call x0 -> x1, Pallas kernels: none -> 102 us  [prefill(): pl.pallas_call(functools.partial(prefill_kernel, plane, groups, direct),...]
    all_gather x1 -> x0, waiting for transfers between devices: 92.1 us -> none  [shards(): lax.all_gather(key_value_weight, 'gx', axis=0, tiled=True)]
    dot_general x1 -> x0, matrix products: 18.6 us -> none  [shards(): jnp.dot(prefix_tokens, lax.all_gather(key_value_weight, 'gx', axis=0, til...]
    all_to_all x1, waiting for transfers between devices: 3.86 us -> 0.01 us  [shards(): lax.all_to_all(attention, 'gy', split_axis=1, concat_axis=0, tiled=True)]
  transfers between devices with their start and end apart: 3 -> 2, of which waited for: 2 -> 0; matrix products, arithmetic and copies ran while one was open for 10% -> 1% of each run, Pallas kernels for 0% -> 53%
where the time goes in v1:
time: 194 us; the launch traced here: 193 us
  Pallas kernels  102 us (53%)
  blocking collectives  46.3 us (24%)
  other arithmetic  16.8 us (9%)
  between operations  14.2 us (7%)
  local copies, waits for them, and re-layouts  5.25 us (3%)
  matrix products  4.21 us (2%)
  starting transfers between devices  3.3 us (2%)
    pallas_call x1, Pallas kernels, prefill(): pl.pallas_call(functools.partial(prefill_kernel, plane, groups, direct),...  102 us
    all_gather x2, blocking collectives, merged(): gathered = jax.tree.map(lambda a: lax.all_gather(a, axis), part)  41.4 us
    add x15, other arithmetic, merge_parts(): earlier[2] * early_factor[..., None] + later[2] * late_factor[..., None]  14.3 us
    psum x1, blocking collectives, shards(): whole = lax.psum(partial_value, 'gy')  4.98 us
  transfers between devices with their start and end apart: 2, of which 0 were waited for; matrix products, arithmetic and copies ran while one was open for 1% of the time, Pallas kernels for 53%

profile of v1, /device:TPU:0, one launch (start us, length us, event | category | flops | bytes accessed | tf_op | source)
XLA Modules:
  0.0 192.5 jit_solution(2394936266010837656)
XLA Ops:
  7.2 0.0 copy-start.4
  7.2 0.0 copy-start.1
  7.2 0.0 copy-start.2
  7.2 0.0 all-gather.5.cloned.1.call-start
  7.3 1.3 fusion.15
  8.5 0.3 copy.22
  8.8 0.0 copy-start
  8.8 0.3 copy.23
  9.1 0.1 broadcast_compare_fusion
  9.2 0.0 copy-done.1
  9.2 0.3 select_reduce_fusion
  9.5 1.1 fusion.6
  10.6 0.0 all-gather.5.cloned.1.call-update
  10.6 23.5 %all-gather = f32[32,8,8]{2,1,0:T(8,128)S(1)} all-gather(f32[2,8,8]{2,1,0:T(8,128)S(1)} %get-tuple-element.204), channel_id=2, replica_groups=mesh['gx'=16,'gy'=2] {'gx'}, dimensions={0}, use_global_device_ids=true | all-gather | bytes 8704 | tf_op jit(solution)/shard_map/all_gather | solution.py:22
  34.1 0.2 fusion.5
  34.3 17.9 %all-gather.1 = f32[32,8,8]{2,1,0:T(8,128)S(1)} all-gather(f32[2,8,8]{2,1,0:T(8,128)S(1)} %fusion.5), channel_id=3, replica_groups=mesh['gx'=16,'gy'=2] {'gx'}, dimensions={0}, use_global_device_ids=true | all-gather | bytes 8704 | tf_op jit(solution)/shard_map/all_gather | solution.py:22
  52.2 0.1 convert_bitcast_fusion.1
  52.2 0.1 convert_bitcast_fusion
  52.3 1.4 fusion.3
  53.8 0.0 all-gather.5.cloned.1.call-done
  53.8 0.8 slice.16
  54.6 15.1 %while.19 = (s32[]{:T(128)}, f32[2,8,8]{2,1,0:T(8,128)S(1)}, f32[2,8,8]{2,1,0:T(8,128)S(1)}, f32[2,8,8,128]{3,2,1,0:T(8,128)S(1)}, f32[16,2,8,8]{3,2,1,0:T(8,128...) while((s32[]{:T(128)}, f32[2,8,8]{2,1,0:T(8,128)S(1)}, ...), condition=%wide.region_3.4_spmd, body=%wide.region_2.3_spmd.sunk | while | flops 49925 | bytes 201879 | solution.py:27
  54.6 1.0 fusion.24
  55.7 1.0 fusion.24
  56.7 1.0 fusion.24
  57.7 1.0 fusion.24
  58.7 1.0 fusion.24
  59.7 1.0 fusion.24
  60.7 1.0 fusion.24
  61.7 1.0 fusion.24
  62.7 1.0 fusion.24
  63.7 1.0 fusion.24
  64.7 1.0 fusion.24
  65.7 1.0 fusion.24
  66.7 1.0 fusion.24
  67.7 1.0 fusion.24
  68.8 1.0 fusion.24
  69.7 0.1 divide_convert_fusion
  69.8 0.6 copy.19
  70.5 3.3 %all-to-all-start = ((bf16[2,2,4096]{2,0,1:T(2,128)(2,1)}), bf16[2,2,4096]{2,0,1:T(2,128)(2,1)S(1)}, u32[]{:S(2)}, u32[]{:S(2)}) async-start(bf16[2,2,4096]{2,0,1:T(2,128)(2,1)} %copy.19), calls=%async_computation | async-start | bytes 65536 | tf_op jit(solution)/shard_map/all_to_all | solution.py:405
  73.8 0.3 pad_maximum_fusion
  74.0 0.2 broadcast_in_dim.40.mask_ref
  74.2 101.9 %prefill.1 = bf16[768,1024]{1,0:T(8,128)(2,1)S(1)} custom-call(bf16[768,8192]{1,0:T(8,128)(2,1)} %x_hbm.1, bf16[512,1024]{1,0:T(8,128)(2,1)S(1)} %copy-done, f32[768,128]{1,0:T(8,128)S(1)} %get-tuple-element.206.cos_ref, f32[768,128]{1,0:T(8,128)S(1)} %get-tuple-element.207.sin_ref, f32[768,128]{1,0:T(8,128)S(1)} %broadcast_in_dim.40.mask_ref), custom_call_target="tpu_custom_call" | custom-call | tf_op jit(solution)/shard_map/prefill/pallas_call | solution.py:331
  176.1 0.0 all-to-all-done
  176.1 2.8 %fusion.16 = f32[4,512]{1,0:T(4,128)S(1)} fusion(bf16[4,4096]{1,0:T(4,128)(2,1)S(1)} %all_to_all.14, bf16[4096,512]{1,0:T(8,128)(2,1)} %param.17), kind=kOutput, calls=%fused_computation.34 | convolution fusion | flops 16777216 | bytes 4235264 | tf_op jit(solution)/shard_map/dot_general | solution.py:406
  179.0 5.0 %psum.7 = bf16[4,512]{1,0:T(4,128)(2,1)S(1)} all-reduce(f32[4,512]{1,0:T(4,128)S(1)} %fusion.16), channel_id=1, replica_groups=mesh['gx'=16,'gy'=2] {'gy'}, use_global_device_ids=true, to_apply=%region_4.5 | all-reduce | flops 2048 | bytes 12288 | tf_op jit(solution)/shard_map/psum | solution.py:407
  183.9 0.6 dynamic-slice_convert_fusion
  184.5 1.1 copy.44
  (26 shorter events, 0.3 us)
Async XLA Ops:
  7.2 1.9 %copy-start.4 = (s32[2]{0:T(128)S(1)}, s32[2]{0:T(128)}, u32[]{:S(2)}) copy-start(s32[2]{0:T(128)} %param.16) | copy-start | bytes 28
  7.2 2.0 %copy-start.1 = (bf16[2,8192]{1,0:T(2,128)(2,1)S(1)}, bf16[2,8192]{1,0:T(2,128)(2,1)}, u32[]{:S(2)}) copy-start(bf16[2,8192]{1,0:T(2,128)(2,1)} %param.14) | copy-start | bytes 98308
  7.2 45.0 %copy-start.2 = (s32[6]{0:T(128)S(1)}, s32[6]{0:T(128)}, u32[]{:S(2)}) copy-start(s32[6]{0:T(128)} %param.13) | copy-start | bytes 76
  7.2 45.0 %copy-start.3 = (s32[6]{0:T(128)S(1)}, s32[6]{0:T(128)}, u32[]{:S(2)}) copy-start(s32[6]{0:T(128)} %param.12) | copy-start | bytes 76
  7.2 46.6 %all-gather.5.cloned.1.call-start = ((), (), s32[]{:S(2)}) async-start(), calls=%async_computation.1 | async-start | bytes 1114112 | tf_op jit(solution)/shard_map/all_gather | solution.py:22
  8.8 65.4 %copy-start = (bf16[512,1024]{1,0:T(8,128)(2,1)S(1)}, bf16[512,1024]{1,0:T(8,128)(2,1)}, u32[]{:S(2)}) copy-start(bf16[512,1024]{1,0:T(8,128)(2,1)} %w_hbm.1) | copy-start | bytes 3145732
  70.5 105.6 %all-to-all-start = ((bf16[2,2,4096]{2,0,1:T(2,128)(2,1)}), bf16[2,2,4096]{2,0,1:T(2,128)(2,1)S(1)}, u32[]{:S(2)}, u32[]{:S(2)}) async-start(bf16[2,2,4096]{2,0,1:T(2,128)(2,1)} %copy.19), calls=%async_computation | async-start | bytes 65536 | tf_op jit(solution)/shard_map/all_to_all | solution.py:405
Sparse Core Ops, SparseCore 0:
  10.7 40.7 all-gather.4

commit v2 on v1

--- a/solution.py
+++ b/solution.py
@@ -16,17 +16,6 @@
 
 rope_base = 500000.0
 masked_score = -1e30
-
-
-def merged(part, axis, combine):
-    gathered = jax.tree.map(lambda a: lax.all_gather(a, axis), part)
-
-    def take(source):
-        return jax.tree.map(lambda a: lax.dynamic_index_in_dim(a, source, 0, False), gathered)
-
-    return lax.fori_loop(
-        1, lax.axis_size(axis), lambda source, state: combine(state, take(source)), take(0)
-    )
 
 
 def plane_of(mesh):
@@ -351,13 +340,172 @@
     )(tokens, weight, cosine, sine, mask)
 
 
-def merge_parts(earlier, later):
-    highest = jnp.maximum(earlier[0], later[0])
-    early_factor = jnp.exp(earlier[0] - highest)
-    late_factor = jnp.exp(later[0] - highest)
-    summed = earlier[1] * early_factor + later[1] * late_factor
-    weighted = earlier[2] * early_factor[..., None] + later[2] * late_factor[..., None]
-    return (highest, summed, weighted)
+def decode_kernel(
+    sizes, part_ref, w_hbm, o_ref,
+    got, mine, spread, laid, wbuf, terms, red,
+    w_sem, send1, recv1, send2, recv2, send3, recv3,
+):
+    n, lanes, batch, heads, near = sizes
+    me = lax.axis_index("gx")
+    side = lax.axis_index("gy")
+    rows = batch * heads
+    per_side = near // heads
+    home = lax.div(me, per_side)
+    slot = lax.rem(me, per_side)
+
+    def each(low, high, body):
+        lax.fori_loop(low, high, lambda i, s: (body(i), s)[1], 0)
+
+    load = pltpu.make_async_copy(w_hbm, wbuf, w_sem)
+    load.start()
+
+    def scatter(step):
+        to = lax.rem(me + step, n)
+        return pltpu.make_async_remote_copy(
+            src_ref=part_ref.at[to], dst_ref=got.at[me], send_sem=send1.at[step],
+            recv_sem=recv1.at[me], device_id={"gx": to}, device_id_type=MESH,
+        )
+
+    def scattered(source):
+        return pltpu.make_async_remote_copy(
+            src_ref=part_ref.at[0], dst_ref=got.at[source], send_sem=send1.at[0],
+            recv_sem=recv1.at[source], device_id={"gx": source}, device_id_type=MESH,
+        )
+
+    each(1, n, lambda step: scatter(step).start())
+    got[me] = part_ref[me]
+    each(1, n, lambda step: scattered(lax.rem(me + step, n)).wait_recv())
+    top = lax.fori_loop(
+        0, n, lambda i, t: jnp.maximum(t, got[i, rows : 2 * rows, :]), jnp.full((rows, HEAD_SIZE), masked_score)
+    )
+
+    def add(i, state):
+        total, combined = state
+        factor = jnp.exp(got[i, rows : 2 * rows, :] - top)
+        return total + got[i, 2 * rows :, :] * factor, combined + got[i, :rows, :] * factor
+
+    nothing = jnp.zeros((rows, HEAD_SIZE), jnp.float32)
+    total, combined = lax.fori_loop(0, n, add, (nothing, nothing))
+    attention = (combined / total).astype(jnp.bfloat16).astype(jnp.float32)
+    mine[...] = attention
+
+    def hand(to):
+        return pltpu.make_async_remote_copy(
+            src_ref=mine, dst_ref=spread.at[side, slot], send_sem=send2.at[to],
+            recv_sem=recv2.at[side, slot], device_id={"gx": to, "gy": home}, device_id_type=MESH,
+        )
+
+    def others(act):
+        def one(step):
+            to = lax.rem(me + step, n)
+
+            @pl.when(jnp.logical_or(step > 0, home != side))
+            def _():
+                act(hand(to))
+
+        each(0, n, one)
+
+    others(lambda copy: copy.start())
+
+    @pl.when(home == side)
+    def _():
+        spread[side, slot] = attention
+
+    def take(i):
+        s, j = lax.div(i, per_side), lax.rem(i, per_side)
+        source = side * per_side + j
+
+        @pl.when(jnp.logical_or(s != side, source != me))
+        def _():
+            pltpu.make_async_remote_copy(
+                src_ref=mine, dst_ref=spread.at[s, j], send_sem=send2.at[0],
+                recv_sem=recv2.at[s, j], device_id={"gx": source, "gy": s}, device_id_type=MESH,
+            ).wait_recv()
+
+    each(0, lanes * per_side, take)
+    for s in range(lanes):
+        for j in range(per_side):
+            for b in range(batch):
+                for k in range(heads):
+                    at = (j * heads + k) * HEAD_SIZE
+                    laid[s * batch + b : s * batch + b + 1, at : at + HEAD_SIZE] = spread[
+                        s, j, b * heads + k : b * heads + k + 1, :
+                    ]
+    load.wait()
+    partial_value = jnp.dot(
+        laid[...].astype(jnp.bfloat16), wbuf[...], preferred_element_type=jnp.float32
+    )
+    for s in range(lanes):
+        terms[s] = partial_value[s * batch : (s + 1) * batch, :]
+
+    def give(step):
+        to = lax.rem(side + step, lanes)
+        return pltpu.make_async_remote_copy(
+            src_ref=terms.at[to], dst_ref=red.at[side], send_sem=send3.at[step],
+            recv_sem=recv3.at[side], device_id={"gy": to}, device_id_type=MESH,
+        )
+
+    def given(step):
+        source = lax.rem(side + step, lanes)
+        return pltpu.make_async_remote_copy(
+            src_ref=terms.at[0], dst_ref=red.at[source], send_sem=send3.at[0],
+            recv_sem=recv3.at[source], device_id={"gy": source}, device_id_type=MESH,
+        )
+
+    each(1, lanes, lambda step: give(step).start())
+    red[side] = terms[side]
+    each(1, lanes, lambda step: given(step).wait_recv())
+    whole = red[0]
+    for s in range(1, lanes):
+        whole = whole + red[s]
+    o_ref[...] = whole.astype(o_ref.dtype)
+    each(1, n, lambda step: scatter(step).wait_send())
+    others(lambda copy: copy.wait_send())
+    each(1, lanes, lambda step: give(step).wait_send())
+
+
+def decode(sizes, peak, block_total, numerator, out_weight):
+    n, lanes, batch, heads, near = sizes
+
+    def by_owner(a):
+        a = jnp.broadcast_to(a, (batch, KEY_VALUE_HEADS, QUERY_HEADS // KEY_VALUE_HEADS, HEAD_SIZE))
+        a = a.reshape(batch, n, heads, HEAD_SIZE).transpose(1, 0, 2, 3)
+        return a.reshape(n, batch * heads, HEAD_SIZE)
+
+    parts = jnp.concatenate(
+        [by_owner(numerator), by_owner(peak[..., None]), by_owner(block_total[..., None])], axis=1
+    )
+    rows = batch * heads
+    depth, columns = out_weight.shape
+    per_side = near // heads
+    vmem = pl.BlockSpec(memory_space=pltpu.VMEM)
+    dma = pltpu.SemaphoreType.DMA
+    return pl.pallas_call(
+        functools.partial(decode_kernel, sizes),
+        out_shape=jax.ShapeDtypeStruct((batch, columns), jnp.bfloat16),
+        in_specs=[vmem, pl.BlockSpec(memory_space=pl.ANY)],
+        out_specs=vmem,
+        scratch_shapes=[
+            pltpu.VMEM((n, 3 * rows, HEAD_SIZE), jnp.float32),
+            pltpu.VMEM((rows, HEAD_SIZE), jnp.float32),
+            pltpu.VMEM((lanes, per_side, rows, HEAD_SIZE), jnp.float32),
+            pltpu.VMEM((lanes * batch, depth), jnp.float32),
+            pltpu.VMEM((depth, columns), jnp.bfloat16),
+            pltpu.VMEM((lanes, batch, columns), jnp.float32),
+            pltpu.VMEM((lanes, batch, columns), jnp.float32),
+            dma(()),
+            dma((n,)),
+            dma((n,)),
+            dma((n,)),
+            dma((lanes, per_side)),
+            dma((lanes,)),
+            dma((lanes,)),
+        ],
+        compiler_params=pltpu.CompilerParams(
+            has_side_effects=True, vmem_limit_bytes=24 * 1024 * 1024
+        ),
+        name="decode",
+    )(parts, out_weight)
 
 
 def shards(
@@ -396,19 +544,12 @@
         value_rows,
         preferred_element_type=jnp.float32,
     )
-    peak, block_total, numerator = merged((peak, block_total, numerator), "gx", merge_parts)
-    attention = (
-        (numerator / block_total[..., None])
-        .reshape(trajectory_per_shard, QUERY_HEADS * HEAD_SIZE)
-        .astype(jnp.bfloat16)
-    )
-    spread = lax.all_to_all(attention, "gy", split_axis=1, concat_axis=0, tiled=True)
-    partial_value = jnp.dot(spread, out_weight, preferred_element_type=jnp.float32)
-    whole = lax.psum(partial_value, "gy")
-    mixed = lax.dynamic_slice_in_dim(
-        whole, lax.axis_index("gy") * trajectory_per_shard, trajectory_per_shard, 0
-    )
-    return (prefix_kv, mixed.astype(jnp.bfloat16))
+    n = lax.axis_size("gx")
+    sizes = (
+        n, lax.axis_size("gy"), trajectory_per_shard, QUERY_HEADS // n, out_weight.shape[0] // HEAD_SIZE
+    )
+    decode_out = decode(sizes, peak, block_total, numerator, out_weight)
+    return (prefix_kv, decode_out)
 
 
 def solution(mesh):

time: 194 us -> 136 us (0.70)
  blocking collectives: 46.3 us -> 0 us
  Pallas kernels: 102 us -> 125 us
  between operations: 14.2 us -> 0.81 us
  other arithmetic: 16.8 us -> 3.54 us
  matrix products: 4.21 us -> 0.73 us
  starting transfers between devices: 3.3 us -> 0 us
    all_gather x2 -> x0, blocking collectives: 41.4 us -> none  [merged(): gathered = jax.tree.map(lambda a: lax.all_gather(a, axis), part)]
    pallas_call x0 -> x1, Pallas kernels: none -> 19.5 us  [decode(): pl.pallas_call(functools.partial(decode_kernel, sizes), out_shape=jax.Sha...]
    add x30 -> x0, other arithmetic: 14.6 us -> none  [the longest x15 14.3 us: merge_parts(): earlier[2] * early_factor[..., None] + later[2] * late_factor[..., None]]
    psum x1 -> x0, blocking collectives: 4.98 us -> none  [shards(): whole = lax.psum(partial_value, 'gy')]
    pallas_call x1, Pallas kernels: 102 us -> 105 us  [prefill(): pl.pallas_call(functools.partial(prefill_kernel, plane, groups, direct),...]
    all_to_all x1 -> x0, starting transfers between devices: 3.26 us -> none  [shards(): lax.all_to_all(attention, 'gy', split_axis=1, concat_axis=0, tiled=True)]
    dot_general x1 -> x0, matrix products: 2.83 us -> none  [shards(): jnp.dot(spread, out_weight, preferred_element_type=jnp.float32)]
    unnamed x13 -> x12, local copies, waits for them, and re-layouts: 1.7 us -> 4.47 us
  transfers between devices with their start and end apart: 2 -> 0, of which waited for: 0 -> 0; matrix products, arithmetic and copies ran while one was open for 1% -> 0% of each run, Pallas kernels for 53% -> 0%
where the time goes in v2:
time: 136 us
  Pallas kernels  125 us (92%)
  local copies, waits for them, and re-layouts  6.26 us (5%)
  other arithmetic  3.54 us (3%)
    pallas_call x1, Pallas kernels, prefill(): pl.pallas_call(functools.partial(prefill_kernel, plane, groups, direct),...  105 us
    pallas_call x1, Pallas kernels, decode(): pl.pallas_call(functools.partial(decode_kernel, sizes), out_shape=jax.Sha...  19.5 us
    unnamed x12, local copies, waits for them, and re-layouts  4.47 us

profile of v2, /device:TPU:0, one launch (start us, length us, event | category | flops | bytes accessed | tf_op | source)
XLA Modules:
  0.0 136.2 jit_solution(1795836498157407467)
XLA Ops:
  0.6 0.0 copy-start.1
  0.7 0.8 convert_bitcast_fusion.1
  1.5 1.4 %fusion = (f32[768,64]{1,0:T(8,128)S(1)}, f32[768,64]{1,0:T(8,128)S(1)}, f32[768,64]{1,0:T(8,128)S(1)}) fusion(f32[64]{0:T(128)S(1)} %multiply_power_fusion, f32[768]{0:T(1024)S(1)} %convert_bitcast_fusion.1), kind=kLoop, calls=%fused_computation.6 | loop fusion | flops 98304 | bytes 593152 | tf_op jit(solution)/shard_map/neg | solution.py:314
  2.9 0.3 pad_maximum_fusion
  3.2 0.7 convert_bitcast_fusion
  3.9 0.2 broadcast_in_dim.24.mask_ref
  4.1 0.0 copy-done.1
  4.1 0.0 copy-start.3
  4.1 0.0 copy-start.2
  4.1 105.4 %prefill.1 = bf16[768,1024]{1,0:T(8,128)(2,1)S(1)} custom-call(bf16[768,8192]{1,0:T(8,128)(2,1)} %x_hbm.1, bf16[512,1024]{1,0:T(8,128)(2,1)S(1)} %copy-done.1, f32[768,128]{1,0:T(8,128)S(1)} %get-tuple-element.9.cos_ref, f32[768,128]{1,0:T(8,128)S(1)} %get-tuple-element.10.sin_ref, f32[768,128]{1,0:T(8,128)S(1)} %broadcast_in_dim.24.mask_ref), custom_call_target="tpu_custom_call" | custom-call | tf_op jit(solution)/shard_map/prefill/pallas_call | solution.py:320
  109.6 0.0 copy-done.3
  109.6 0.1 broadcast_compare_fusion
  109.6 1.3 fusion.11
  110.9 0.3 copy.22
  111.2 0.0 copy-done.2
  111.2 0.3 select_reduce_fusion
  111.5 0.2 fusion.1
  111.7 0.1 broadcast_in_dim.28
  111.8 0.1 broadcast_in_dim.50
  111.9 0.1 sub.14
  112.0 0.1 sub.15
  112.1 0.3 copy.23
  112.4 0.4 fusion.3
  112.8 0.0 copy-start
  112.8 2.2 %copy-done = bf16[4096,512]{1,0:T(8,128)(2,1)S(1)} copy-done((bf16[4096,512]{1,0:T(8,128)(2,1)S(1)}, bf16[4096,512]{1,0:T(8,128)(2,1)}, u32[]{:S(2)}) %copy-start) | copy-done | bytes 4194328
  115.0 19.5 %decode.1 = bf16[2,512]{1,0:T(2,128)(2,1)S(1)} custom-call(f32[16,24,128]{2,1,0:T(8,128)S(1)} %pad_maximum_fusion.2.part_ref, bf16[4096,512]{1,0:T(8,128)(2,1)S(1)} %copy-done), custom_call_target="tpu_custom_call" | custom-call | tf_op jit(solution)/shard_map/decode/pallas_call | solution.py:483
  134.5 1.1 copy.33
  135.7 0.6 copy.34
  (6 shorter events, 0.1 us)
Async XLA Ops:
  0.6 3.5 %copy-start.1 = (bf16[512,1024]{1,0:T(8,128)(2,1)S(1)}, bf16[512,1024]{1,0:T(8,128)(2,1)}, u32[]{:S(2)}) copy-start(bf16[512,1024]{1,0:T(8,128)(2,1)} %w_hbm.2) | copy-start | bytes 3145732
  4.1 105.5 %copy-start.3 = (s32[2]{0:T(128)S(1)}, s32[2]{0:T(128)}, u32[]{:S(2)}) copy-start(s32[2]{0:T(128)} %param.14) | copy-start | bytes 28
  4.1 107.1 %copy-start.2 = (bf16[2,8192]{1,0:T(2,128)(2,1)S(1)}, bf16[2,8192]{1,0:T(2,128)(2,1)}, u32[]{:S(2)}) copy-start(bf16[2,8192]{1,0:T(2,128)(2,1)} %param.12) | copy-start | bytes 98308
  112.8 2.2 %copy-start = (bf16[4096,512]{1,0:T(8,128)(2,1)S(1)}, bf16[4096,512]{1,0:T(8,128)(2,1)}, u32[]{:S(2)}) copy-start(bf16[4096,512]{1,0:T(8,128)(2,1)} %w_hbm.3) | copy-start | bytes 12582916

commit v3 on v1

--- a/solution.py
+++ b/solution.py
@@ -16,17 +16,6 @@
 
 rope_base = 500000.0
 masked_score = -1e30
-
-
-def merged(part, axis, combine):
-    gathered = jax.tree.map(lambda a: lax.all_gather(a, axis), part)
-
-    def take(source):
-        return jax.tree.map(lambda a: lax.dynamic_index_in_dim(a, source, 0, False), gathered)
-
-    return lax.fori_loop(
-        1, lax.axis_size(axis), lambda source, state: combine(state, take(source)), take(0)
-    )
 
 
 def plane_of(mesh):
@@ -44,10 +33,178 @@
     return n // row, row // nc, nc
 
 
-def prefill_kernel(
-    plane, groups, direct, x_hbm, w_hbm, cos_ref, sin_ref, mask_ref, o_ref,
-    xbuf, wbuf, x_sem, own_sem, recv_sem, up_sem, down_sem, cross_sem, core_sem,
+def decode_phases(
+    sizes, part_ref, w_hbm, o_ref,
+    got, mine, spread, laid, wbuf, terms, red,
+    w_sem, send1, recv1, send2, recv2, send3, recv3,
 ):
+    n, lanes, batch, heads, near = sizes
+    me = lax.axis_index("gx")
+    side = lax.axis_index("gy")
+    rows = batch * heads
+    per_side = near // heads
+    home = lax.div(me, per_side)
+    slot = lax.rem(me, per_side)
+
+    def each(low, high, body):
+        lax.fori_loop(low, high, lambda i, s: (body(i), s)[1], 0)
+
+    load = pltpu.make_async_copy(w_hbm, wbuf, w_sem)
+
+    def scatter(step):
+        to = lax.rem(me + step, n)
+        return pltpu.make_async_remote_copy(
+            src_ref=part_ref.at[to], dst_ref=got.at[me], send_sem=send1.at[step],
+            recv_sem=recv1.at[me], device_id={"gx": to}, device_id_type=MESH,
+        )
+
+    def scattered(source):
+        return pltpu.make_async_remote_copy(
+            src_ref=part_ref.at[0], dst_ref=got.at[source], send_sem=send1.at[0],
+            recv_sem=recv1.at[source], device_id={"gx": source}, device_id_type=MESH,
+        )
+
+    def begin():
+        load.start()
+        each(1, n, lambda step: scatter(step).start())
+
+    def hand(to):
+        return pltpu.make_async_remote_copy(
+            src_ref=mine, dst_ref=spread.at[side, slot], send_sem=send2.at[to],
+            recv_sem=recv2.at[side, slot], device_id={"gx": to, "gy": home}, device_id_type=MESH,
+        )
+
+    def others(act):
+        def one(step):
+            to = lax.rem(me + step, n)
+
+            @pl.when(jnp.logical_or(step > 0, home != side))
+            def _():
+                act(hand(to))
+
+        each(0, n, one)
+
+    def merge():
+        got[me] = part_ref[me]
+        each(1, n, lambda step: scattered(lax.rem(me + step, n)).wait_recv())
+        top = lax.fori_loop(
+            0, n, lambda i, t: jnp.maximum(t, got[i, rows : 2 * rows, :]), jnp.full((rows, HEAD_SIZE), masked_score)
+        )
+
+        def add(i, state):
+            total, combined = state
+            factor = jnp.exp(got[i, rows : 2 * rows, :] - top)
+            return total + got[i, 2 * rows :, :] * factor, combined + got[i, :rows, :] * factor
+
+        nothing = jnp.zeros((rows, HEAD_SIZE), jnp.float32)
+        total, combined = lax.fori_loop(0, n, add, (nothing, nothing))
+        attention = (combined / total).astype(jnp.bfloat16).astype(jnp.float32)
+        mine[...] = attention
+
+        others(lambda copy: copy.start())
+
+        @pl.when(home == side)
+        def _():
+            spread[side, slot] = attention
+
+    def take(i):
+        s, j = lax.div(i, per_side), lax.rem(i, per_side)
+        source = side * per_side + j
+
+        @pl.when(jnp.logical_or(s != side, source != me))
+        def _():
+            pltpu.make_async_remote_copy(
+                src_ref=mine, dst_ref=spread.at[s, j], send_sem=send2.at[0],
+                recv_sem=recv2.at[s, j], device_id={"gx": source, "gy": s}, device_id_type=MESH,
+            ).wait_recv()
+
+    def give(step):
+        to = lax.rem(side + step, lanes)
+        return pltpu.make_async_remote_copy(
+            src_ref=terms.at[to], dst_ref=red.at[side], send_sem=send3.at[step],
+            recv_sem=recv3.at[side], device_id={"gy": to}, device_id_type=MESH,
+        )
+
+    def given(step):
+        source = lax.rem(side + step, lanes)
+        return pltpu.make_async_remote_copy(
+            src_ref=terms.at[0], dst_ref=red.at[source], send_sem=send3.at[0],
+            recv_sem=recv3.at[source], device_id={"gy": source}, device_id_type=MESH,
+        )
+
+    def project():
+        each(0, lanes * per_side, take)
+        for s in range(lanes):
+            for j in range(per_side):
+                for b in range(batch):
+                    for k in range(heads):
+                        at = (j * heads + k) * HEAD_SIZE
+                        laid[s * batch + b : s * batch + b + 1, at : at + HEAD_SIZE] = spread[
+                            s, j, b * heads + k : b * heads + k + 1, :
+                        ]
+        load.wait()
+        partial_value = jnp.dot(
+            laid[...].astype(jnp.bfloat16), wbuf[...], preferred_element_type=jnp.float32
+        )
+        for s in range(lanes):
+            terms[s] = partial_value[s * batch : (s + 1) * batch, :]
+        each(1, lanes, lambda step: give(step).start())
+        red[side] = terms[side]
+
+    def end():
+        each(1, lanes, lambda step: given(step).wait_recv())
+        whole = red[0]
+        for s in range(1, lanes):
+            whole = whole + red[s]
+        o_ref[...] = whole.astype(o_ref.dtype)
+
+    def drain():
+        each(1, n, lambda step: scatter(step).wait_send())
+        others(lambda copy: copy.wait_send())
+        each(1, lanes, lambda step: give(step).wait_send())
+
+    return begin, merge, project, end, drain
+
+
+def decode_parts(sizes, peak, block_total, numerator, out_weight):
+    n, lanes, batch, heads, near = sizes
+
+    def by_owner(a):
+        a = jnp.broadcast_to(a, (batch, KEY_VALUE_HEADS, QUERY_HEADS // KEY_VALUE_HEADS, HEAD_SIZE))
+        a = a.reshape(batch, n, heads, HEAD_SIZE).transpose(1, 0, 2, 3)
+        return a.reshape(n, batch * heads, HEAD_SIZE)
+
+    parts = jnp.concatenate(
+        [by_owner(numerator), by_owner(peak[..., None]), by_owner(block_total[..., None])], axis=1
+    )
+    rows = batch * heads
+    depth, columns = out_weight.shape
+    per_side = near // heads
+    dma = pltpu.SemaphoreType.DMA
+    scratch = [
+        pltpu.VMEM((n, 3 * rows, HEAD_SIZE), jnp.float32),
+        pltpu.VMEM((rows, HEAD_SIZE), jnp.float32),
+        pltpu.VMEM((lanes, per_side, rows, HEAD_SIZE), jnp.float32),
+        pltpu.VMEM((lanes * batch, depth), jnp.float32),
+        pltpu.VMEM((depth, columns), jnp.bfloat16),
+        pltpu.VMEM((lanes, batch, columns), jnp.float32),
+        pltpu.VMEM((lanes, batch, columns), jnp.float32),
+        dma(()),
+        dma((n,)),
+        dma((n,)),
+        dma((n,)),
+        dma((lanes, per_side)),
+        dma((lanes,)),
+        dma((lanes,)),
+    ]
+    return parts, scratch
+
+
+def layer_kernel(
+    plane, sizes, groups, direct, x_hbm, w_hbm, cos_ref, sin_ref, mask_ref, part_ref, ow_hbm, o_ref, d_ref,
+    xbuf, wbuf, x_sem, own_sem, recv_sem, up_sem, down_sem, cross_sem, core_sem, *decode_refs,
+):
+    begin, merge, project, end, drain = decode_phases(sizes, part_ref, ow_hbm, d_ref, *decode_refs)
     nz, nx, nc = plane
     me = lax.axis_index("gx")
     key_groups = KEY_VALUE_HEADS - lax.axis_index("gy") * groups
@@ -111,26 +268,7 @@
     each(0, travelled, lambda g: own_copy(g).start())
     x_copy.start()
 
-    barrier = pltpu.get_barrier_semaphore()
-
-    def greet(target):
-        pl.semaphore_signal(barrier, inc=1, device_id={"gx": target}, device_id_type=MESH)
-
-    @pl.when(z > 0)
-    def _():
-        greet(index(z - 1, x, c))
-
-    @pl.when(z < nz - 1)
-    def _():
-        greet(index(z + 1, x, c))
-
-    for step in range(1, nx):
-        greet(index(z, lax.rem(x + step, nx), c))
-    for step in range(1, nc):
-        greet(index(z, x, lax.rem(c + step, nc)))
-
-    peers = nx + nc - 2 + jnp.where(z > 0, 1, 0) + jnp.where(z < nz - 1, 1, 0)
-    pl.semaphore_wait(barrier, peers)
+    begin()
 
     def send_own(g, act):
         send_up(g, me, act)
@@ -227,9 +365,10 @@
     x_copy.wait()
 
     def step(g):
-        @pl.when(g + ahead < travelled)
-        def _():
-            ready_own(g + ahead)
+        if travelled > 5:
+            pl.when(g == 1)(merge)
+            pl.when(g == 3)(project)
+            pl.when(g == 5)(end)
 
         @pl.when(g >= 2)
         def _():
@@ -249,20 +388,28 @@
 
         each(1, nz, hop)
 
-        @pl.when(g >= 2)
-        def _():
-            each(min(nz - 1, tiles), tiles, lambda r: multiply(g - 2, r))
-
-        @pl.when(g >= 1)
-        def _():
-            take_x(g - 1)
+        @pl.when(g + ahead < travelled)
+        def _():
+            ready_own(g + ahead)
 
         if direct:
             @pl.when(g < (nz - 1) * nx)
             def _():
                 direct_z(g, start, True)
 
+        @pl.when(g >= 2)
+        def _():
+            each(min(nz - 1, tiles), tiles, lambda r: multiply(g - 2, r))
+
+        @pl.when(g >= 1)
+        def _():
+            take_x(g - 1)
+
     each(0, travelled, step)
+    if travelled <= 5:
+        merge()
+        project()
+        end()
 
     def whole(g):
         take_core(g)
@@ -280,7 +427,6 @@
     if direct:
         order_low = max(travelled - 2, 0)
         def closing(i):
-            g = lax.rem(i + 1, 3)
             g = jnp.where(i == 0, last, order_low + i - 1)
             @pl.when(i == 2)
             def _():
@@ -305,9 +451,10 @@
         send_own(last, finish)
         direct_first(finish, False)
         each(0, (nz - 1) * nx, lambda s: direct_z(s, finish, False))
-
-
-def prefill(plane, tokens, weight, prefix_lengths, start_offsets):
+    drain()
+
+
+def layer(plane, sizes, tokens, weight, prefix_lengths, start_offsets, peak, block_total, numerator, out_weight):
     nz, nx, nc = plane
     n = nz * nx * nc
     rows = tokens.shape[0]
@@ -324,15 +471,19 @@
     cosine = jnp.concatenate([cosine, cosine], axis=1)
     sine = jnp.concatenate([-sine, sine], axis=1)
     mask = jnp.broadcast_to(live[:, None], (rows, HEAD_SIZE)).astype(jnp.float32)
+    parts, decode_scratch = decode_parts(sizes, peak, block_total, numerator, out_weight)
     chips = nz * nx
     vmem = pl.BlockSpec(memory_space=pltpu.VMEM)
     anywhere = pl.BlockSpec(memory_space=pl.ANY)
     dma = pltpu.SemaphoreType.DMA
     return pl.pallas_call(
-        functools.partial(prefill_kernel, plane, groups, direct),
-        out_shape=jax.ShapeDtypeStruct((rows, columns), jnp.bfloat16),
-        in_specs=[anywhere, anywhere, vmem, vmem, vmem],
-        out_specs=vmem,
+        functools.partial(layer_kernel, plane, sizes, groups, direct),
+        out_shape=(
+            jax.ShapeDtypeStruct((rows, columns), jnp.bfloat16),
+            jax.ShapeDtypeStruct((sizes[2], out_weight.shape[1]), jnp.bfloat16),
+        ),
+        in_specs=[anywhere, anywhere, vmem, vmem, vmem, vmem, anywhere],
+        out_specs=(vmem, vmem),
         scratch_shapes=[
             pltpu.VMEM(tokens.shape, jnp.bfloat16),
             pltpu.VMEM((groups, n * depth, HEAD_SIZE), jnp.bfloat16),
@@ -343,21 +494,13 @@
             dma((groups, chips)),
             dma((groups, chips, max(nx - 1, 1))),
             dma((groups, chips, max(nc - 1, 1))),
+            *decode_scratch,
         ],
         compiler_params=pltpu.CompilerParams(
-            collective_id=0, has_side_effects=True, vmem_limit_bytes=48 * 1024 * 1024
+            has_side_effects=True, vmem_limit_bytes=48 * 1024 * 1024
         ),
-        name="prefill",
-    )(tokens, weight, cosine, sine, mask)
-
-
-def merge_parts(earlier, later):
-    highest = jnp.maximum(earlier[0], later[0])
-    early_factor = jnp.exp(earlier[0] - highest)
-    late_factor = jnp.exp(later[0] - highest)
-    summed = earlier[1] * early_factor + later[1] * late_factor
-    weighted = earlier[2] * early_factor[..., None] + later[2] * late_factor[..., None]
-    return (highest, summed, weighted)
+        name="layer",
+    )(tokens, weight, cosine, sine, mask, parts, out_weight)
 
 
 def shards(
@@ -371,7 +514,6 @@
     cache_lengths,
     out_weight,
 ):
-    prefix_kv = prefill(plane, prefix_tokens, key_value_weight, prefix_lengths, start_offsets)
     trajectory_per_shard = queries.shape[0]
     cache_per_shard = key_value_cache.shape[2]
     query_group = QUERY_HEADS // KEY_VALUE_HEADS
@@ -396,19 +538,14 @@
         value_rows,
         preferred_element_type=jnp.float32,
     )
-    peak, block_total, numerator = merged((peak, block_total, numerator), "gx", merge_parts)
-    attention = (
-        (numerator / block_total[..., None])
-        .reshape(trajectory_per_shard, QUERY_HEADS * HEAD_SIZE)
-        .astype(jnp.bfloat16)
-    )
-    spread = lax.all_to_all(attention, "gy", split_axis=1, concat_axis=0, tiled=True)
-    partial_value = jnp.dot(spread, out_weight, preferred_element_type=jnp.float32)
-    whole = lax.psum(partial_value, "gy")
-    mixed = lax.dynamic_slice_in_dim(
-        whole, lax.axis_index("gy") * trajectory_per_shard, trajectory_per_shard, 0
-    )
-    return (prefix_kv, mixed.astype(jnp.bfloat16))
+    n = lax.axis_size("gx")
+    sizes = (
+        n, lax.axis_size("gy"), trajectory_per_shard, QUERY_HEADS // n, out_weight.shape[0] // HEAD_SIZE
+    )
+    return layer(
+        plane, sizes, prefix_tokens, key_value_weight, prefix_lengths, start_offsets,
+        peak, block_total, numerator, out_weight,
+    )
 
 
 def solution(mesh):

time: 194 us -> 126 us (0.65)
  blocking collectives: 46.3 us -> 0 us
  Pallas kernels: 102 us -> 116 us
  between operations: 14.2 us -> 0.76 us
  other arithmetic: 16.8 us -> 4.12 us
  matrix products: 4.21 us -> 0.74 us
  starting transfers between devices: 3.3 us -> 0 us
    all_gather x2 -> x0, blocking collectives: 41.4 us -> none  [merged(): gathered = jax.tree.map(lambda a: lax.all_gather(a, axis), part)]
    add x30 -> x0, other arithmetic: 14.6 us -> none  [the longest x15 14.3 us: merge_parts(): earlier[2] * early_factor[..., None] + later[2] * late_factor[..., None]]
    pallas_call x1, Pallas kernels: 102 us -> 116 us  [layer(): pl.pallas_call(functools.partial(layer_kernel, plane, sizes, groups, dire...]
    psum x1 -> x0, blocking collectives: 4.98 us -> none  [shards(): whole = lax.psum(partial_value, 'gy')]
    all_to_all x1 -> x0, starting transfers between devices: 3.26 us -> none  [shards(): lax.all_to_all(attention, 'gy', split_axis=1, concat_axis=0, tiled=True)]
    dot_general x1 -> x0, matrix products: 2.83 us -> none  [shards(): jnp.dot(spread, out_weight, preferred_element_type=jnp.float32)]
  transfers between devices with their start and end apart: 2 -> 0, of which waited for: 0 -> 0; matrix products, arithmetic and copies ran while one was open for 1% -> 0% of each run, Pallas kernels for 53% -> 0%
where the time goes in v3:
time: 126 us
  Pallas kernels  116 us (92%)
  other arithmetic  4.12 us (3%)
  local copies, waits for them, and re-layouts  4.07 us (3%)
    pallas_call x1, Pallas kernels, layer(): pl.pallas_call(functools.partial(layer_kernel, plane, sizes, groups, dire...  116 us

profile of v3, /device:TPU:0, one launch (start us, length us, event | category | flops | bytes accessed | tf_op | source)
XLA Modules:
  0.0 125.5 jit_solution(4455201578728641852)
XLA Ops:
  0.6 0.0 copy-start.1
  0.7 0.7 broadcast_compare_fusion
  1.4 0.7 convert_bitcast_fusion
  2.1 0.7 convert_bitcast_fusion.1
  2.9 0.2 broadcast_in_dim.24.mask_ref
  3.0 1.3 %fusion.11 = (bf16[1,2,128,1024]{3,2,1,0:T(8,128)(2,1)S(1)}, bf16[1,2,128,1024]{3,2,1,0:T(8,128)(2,1)S(1)}) fusion(bf16[2,2,128,1024]{3,2,1,0:T(8,128)(2,1)} %param.13), kind=kLoop, calls=%fused_computation.24 | loop fusion | bytes 2097152 | tf_op jit(solution)/shard_map/slice | solution.py:524
  4.3 0.0 copy-start
  4.3 0.3 copy.23
  4.6 0.3 copy.22
  4.9 0.0 copy-done.1
  4.9 0.3 select_reduce_fusion
  5.2 0.4 fusion.3
  5.6 0.2 fusion.1
  5.8 0.1 sub.14
  5.9 0.1 broadcast_in_dim.28
  6.0 0.1 broadcast_in_dim.50
  6.1 0.1 sub.15
  6.2 1.4 %fusion = (f32[768,64]{1,0:T(8,128)S(1)}, f32[768,64]{1,0:T(8,128)S(1)}, f32[768,64]{1,0:T(8,128)S(1)}) fusion(f32[64]{0:T(128)S(1)} %multiply_power_fusion, f32[768]{0:T(1024)S(1)} %convert_bitcast_fusion.1), kind=kLoop, calls=%fused_computation.6 | loop fusion | flops 98304 | bytes 593152 | tf_op jit(solution)/shard_map/neg | solution.py:472
  7.7 0.3 pad_maximum_fusion
  7.9 0.0 copy-done
  8.0 115.8 %layer.1 = (bf16[768,1024]{1,0:T(8,128)(2,1)S(1)}, bf16[2,512]{1,0:T(2,128)(2,1)S(1)}) custom-call(bf16[768,8192]{1,0:T(8,128)(2,1)} %x_hbm.1, bf16[512,1024]{1,0:T(8,128)(2,1)S(1)} %copy-done, f32[768,128]{1,0:T(8,128)S(1)} %get-tuple-element.9.cos_ref, f32[768,128]{1,0:T(8,128)S(1)} %get-tuple-element.10.sin_ref, ...), custom_call_target="tpu_custom_call" | custom-call | tf_op jit(solution)/shard_map/layer/pallas_call | solution.py:479
  123.8 1.1 copy.33
  124.9 0.6 copy.34
  (6 shorter events, 0.1 us)
Async XLA Ops:
  0.6 4.2 %copy-start.1 = (bf16[2,8192]{1,0:T(2,128)(2,1)S(1)}, bf16[2,8192]{1,0:T(2,128)(2,1)}, u32[]{:S(2)}) copy-start(bf16[2,8192]{1,0:T(2,128)(2,1)} %param.12) | copy-start | bytes 98308
  4.3 3.7 %copy-start = (bf16[512,1024]{1,0:T(8,128)(2,1)S(1)}, bf16[512,1024]{1,0:T(8,128)(2,1)}, u32[]{:S(2)}) copy-start(bf16[512,1024]{1,0:T(8,128)(2,1)} %w_hbm.1) | copy-start | bytes 3145732
